TPU v7x, 768 devices: a whole 4x8x12 slice. The times are simulated.
768 devices in a mesh: grp: 96 (over x, z, core), sub: 8 (over y).
Axes of the slice: x: 4, y: 8, z: 12, core: 2. Of those that a mesh axis runs over, the one named last changes fastest.
Arguments:
- child_moments: bfloat16 [294, 786432], P(None, ('grp', 'sub')), may hold values from -6 to 6
- upward_matrix: bfloat16 [294, 8, 294], replicated, may hold values from -0.125 to 0.125
- project_matrix: bfloat16 [64, 294], replicated, may hold values from -0.375 to 0.375
- transfer_matrix: bfloat16 [64, 20224], replicated, may hold values from -0.0546875 to 0.0546875
- expand_matrix: bfloat16 [294, 64], replicated, may hold values from -0.75 to 0.75
- downward_matrix: bfloat16 [294, 8, 294], replicated, may hold values from -0.375 to 0.375
- neighbour_list: int32 [316, 98304], P(None, ('grp', 'sub')), may hold values from 0 to 8704, as said below
- ghost_map: int32 [768, 960], P(('grp', 'sub')), may hold values from 0 to 128, as said below
Outputs:
- child_locals: bfloat16 [294, 786432], P(None, ('grp', 'sub'))
Inputs may be any that keep to these rules, and one draw needn't show every extreme that they name: `neighbour_list`: entries below 8704 name a source slot; each column has between 95 and 189 such entries, and the first column of every device's block has exactly 189. Every ghost slot that is named holds a box. `ghost_map`: the groups stand in a three-dimensional arrangement; a device sends boxes only to groups next to its own there (all other destinations hold 128 only). Slot 0 of every such destination names a box, and every device fills all 10 slots of at least one destination.
All inputs are finite; a program needn't handle non-finite values.
Results may differ from a plain program's by a relative error of at most 0.0085.
Values may be sent and summed in bfloat16 or wider, within the bound.
A program may use at most 64 MiB of HBM per device.

v0:
```python
import jax
import jax.numpy as jnp
from jax import lax
from jax.sharding import PartitionSpec as P


def in_order(pieces, dim):
    pieces = jnp.moveaxis(pieces, 0, dim)
    shape = pieces.shape
    return pieces.reshape(*shape[:dim], shape[dim] * shape[dim + 1], *shape[dim + 2 :])


def from_everyone(x, axis):
    copies = jnp.broadcast_to(x, (lax.axis_size(axis), *x.shape))
    return lax.all_to_all(copies, axis, split_axis=0, concat_axis=0, tiled=True)


def gather_directly(x, axis, dim):
    return in_order(from_everyone(x, axis), dim)


def on_device(
    child_moments,
    upward_matrix,
    project_matrix,
    transfer_matrix,
    expand_matrix,
    downward_matrix,
    neighbour_list,
    ghost_map,
):
    surface = child_moments.shape[0]
    box_count = child_moments.shape[1] // 8
    coeff_rows = project_matrix.shape[0]
    children = child_moments.reshape(surface, 8, box_count)
    parent = jnp.einsum(
        "icj,jcb->ib", upward_matrix, children, preferred_element_type=jnp.float32
    ).astype(jnp.bfloat16)
    packed_rows = lax.dot_general(
        parent, project_matrix, (((0,), (1,)), ((), ())), preferred_element_type=jnp.float32
    ).astype(jnp.bfloat16)
    slot_ids = ghost_map.reshape(-1)
    source = jnp.concatenate([packed_rows, jnp.zeros((1, coeff_rows), jnp.bfloat16)], axis=0)[
        slot_ids
    ]
    ghosts = lax.all_to_all(source, "grp", split_axis=0, concat_axis=0, tiled=True)
    mine = jnp.concatenate([packed_rows, ghosts], axis=0)
    sub_count = lax.axis_size("sub")
    ghost_width = ghosts.shape[0]
    width = box_count + ghost_width
    group_boxes = sub_count * box_count
    pool_size = sub_count * width
    lists = jnp.transpose(neighbour_list)
    ghost_index = lists - group_boxes
    own_place = lists // box_count * width + lists % box_count
    ghost_place = ghost_index // ghost_width * width + box_count + ghost_index % ghost_width
    remap = jnp.where(lists < group_boxes, own_place, ghost_place)
    remap = jnp.where(lists < pool_size, remap, -1)
    whole_pool = gather_directly(mine, "sub", 0)
    span = whole_pool.shape[0]
    local = remap - 0
    valid = (local >= 0) & (local < span)
    index = jnp.where(valid, local, span)
    extended = jnp.concatenate([whole_pool, jnp.zeros((1, coeff_rows), jnp.bfloat16)], axis=0)
    picked = extended[index].reshape(box_count, -1)
    local_float = lax.dot_general(
        picked, transfer_matrix, (((1,), (1,)), ((), ())), preferred_element_type=jnp.float32
    )
    local_coeff = local_float.astype(jnp.bfloat16)
    local_moment = lax.dot_general(
        expand_matrix, local_coeff, (((1,), (1,)), ((), ())), preferred_element_type=jnp.float32
    ).astype(jnp.bfloat16)
    result = jnp.einsum(
        "icj,jb->icb", downward_matrix, local_moment, preferred_element_type=jnp.float32
    )
    return result.reshape(surface, 8 * box_count).astype(jnp.bfloat16)


def solution(mesh):
    return jax.shard_map(
        on_device,
        mesh=mesh,
        in_specs=(
            P(None, ("grp", "sub")),
            P(),
            P(),
            P(),
            P(),
            P(),
            P(None, ("grp", "sub")),
            P(("grp", "sub"), None),
        ),
        out_specs=P(None, ("grp", "sub")),
        check_vma=False,
    )
```

profile of v0, /device:TPU:1, one launch (start us, length us, event | category | flops | bytes accessed | tf_op | source)
XLA Modules:
  0.0 189.7 jit_solution(11672540147518332588)
XLA Ops:
  0.0 0.0 copy-start
  0.0 0.8 compare_select_fusion.1
  0.9 0.0 copy-start.3
  0.9 1.2 copy.26
  2.1 4.3 %copy.17 = bf16[294,8,294]{0,1,2:T(8,128)(2,1)} copy(bf16[294,8,294]{2,1,0:T(8,128)(2,1)} %param.9) | data formatting | bytes 2765952 | tf_op args[1]
  6.3 0.0 copy-done.3
  6.3 2.3 %fusion.11 = bf16[128,64]{0,1:T(8,128)(2,1)S(1)} fusion(bf16[64,294]{1,0:T(8,128)(2,1)S(1)} %copy-done.3, bf16[294,8,294]{0,1,2:T(8,128)(2,1)} %copy.17, bf16[296,8,128]{2,1,0:T(8,128)(2,1)S(1)} %bitcast.76), kind=kOutput, calls=%fused_computation.11 | convolution fusion | flops 181883648 | bytes 2050624 | tf_op jit(solution)/shard_map/dot_general | solution.py:39
  8.7 0.1 copy.19
  8.8 3.3 %gather_fusion = bf16[960,64]{1,0:T(8,128)(2,1)S(1)} fusion(bf16[129,64]{1,0:T(8,128)(2,1)S(1)} %concatenate.9.clone, s32[1024]{0:T(1024)S(1)} %pad_clamp_fusion.1), kind=kCustom, calls=%fused_computation | custom fusion | bytes 249600 | tf_op jit(solution)/shard_map/gather | solution.py:43
  12.1 0.1 all_to_all.11
  12.2 0.2 reshape.69
  12.5 34.5 %all_to_all.17 = bf16[96,2,320]{2,1,0:T(2,128)(2,1)S(1)} all-to-all(bf16[96,2,320]{2,1,0:T(2,128)(2,1)S(1)} %reshape.69), channel_id=1, replica_groups=mesh['grp'=96,'sub'=8] {'grp'}, dimensions={0} | all-to-all | bytes 245760 | tf_op jit(solution)/shard_map/all_to_all | solution.py:46
  46.9 0.2 reshape.70
  47.2 0.1 all_to_all.13
  47.3 0.0 copy-start.1
  47.3 0.1 pad_maximum_fusion
  47.4 0.2 copy.20
  47.5 1.2 broadcast_in_dim.10
  48.7 6.8 %all-to-all-start.1 = ((bf16[8,1088,64]{1,2,0:T(8,128)(2,1)}), bf16[8,1088,64]{1,2,0:T(8,128)(2,1)}, u32[]{:S(2)}, u32[]{:S(2)}) async-start(bf16[8,1088,64]{1,2,0:T(8,128)(2,1)} %broadcast_in_dim.10), calls=%async_computation.1 | async-start | bytes 2359296 | tf_op jit(solution)/shard_map/all_to_all | solution.py:15
  55.5 0.0 copy-done.1
  55.5 0.4 compare_select_fusion
  55.9 0.1 copy.22
  56.1 0.2 reshape.58
  56.3 31.3 %all-to-all-done.1 = bf16[8,1088,64]{1,2,0:T(8,128)(2,1)} async-done(((bf16[8,1088,64]{1,2,0:T(8,128)(2,1)}), bf16[8,1088,64]{1,2,0:T(8,128)(2,1)}, u32[]{:S(2)}, u32[]{:S(2)}) %all-to-all-start.1) | async-done | bytes 1114144 | tf_op jit(solution)/shard_map/all_to_all | solution.py:15
  87.6 3.7 %copy.21 = bf16[8,1088,64]{2,1,0:T(8,128)(2,1)} copy(bf16[8,1088,64]{1,2,0:T(8,128)(2,1)} %all-to-all-done.1) | data formatting | bytes 2228224 | tf_op jit(solution)/shard_map/all_to_all | solution.py:15
  91.3 2.8 %concatenate.11 = bf16[8705,64]{1,0:T(8,128)(2,1)} pad(bf16[8704,64]{1,0:T(8,128)(2,1)} %bitcast.73, bf16[]{:T(256)} %constant.45.clone.1), padding=0_1x0_0 | pad | bytes 2228354 | tf_op jit(solution)/shard_map/concatenate | solution.py:64
  94.2 76.6 %gather_fusion.1 = bf16[40448,64]{1,0:T(8,128)(2,1)} fusion(bf16[8705,64]{1,0:T(8,128)(2,1)} %concatenate.11, s32[40960]{0:T(1024)S(1)} %pad_clamp_fusion), kind=kCustom, calls=%fused_computation.1 | custom fusion | bytes 10516480 | tf_op jit(solution)/shard_map/gather | solution.py:65
  170.7 0.0 copy-start.2
  170.7 11.3 %reshape.47 = bf16[128,20224]{1,0:T(8,128)(2,1)} reshape(bf16[40448,64]{1,0:T(8,128)(2,1)} %gather_fusion.1) | data formatting | bytes 10354688 | tf_op jit(solution)/shard_map/reshape | solution.py:65
  182.0 0.0 copy-done
  182.0 0.0 copy-done.2
  182.0 4.5 %fusion.9 = bf16[128,294,1]{0,1,2:T(8,128)(2,1)S(1)} fusion(bf16[294,64]{0,1:T(8,128)(2,1)S(1)} %copy-done.2, bf16[128,20224]{1,0:T(8,128)(2,1)} %reshape.47, bf16[64,20224]{1,0:T(8,128)(2,1)S(1)} %copy-done), kind=kOutput, calls=%fused_computation.9 | convolution fusion | flops 336212736 | bytes 7878912 | tf_op jit(solution)/shard_map/dot_general | solution.py:70
  186.5 2.1 %fusion.5 = bf16[294,8,128]{2,0,1:T(8,128)(2,1)S(1)} fusion(bf16[128,294,1]{0,1,2:T(8,128)(2,1)S(1)} %fusion.9, bf16[294,8,294]{2,1,0:T(8,128)(2,1)} %param.13), kind=kOutput, calls=%fused_computation.5 | convolution fusion | flops 177321984 | bytes 2060352 | tf_op jit(solution)/shard_map/icj,jb->icb/dot_general | solution.py:73
  188.7 0.1 copy.24
  188.8 0.9 copy.27
  (4 shorter events, 0.1 us)
Async XLA Ops:
  0.0 182.0 %copy-start = (bf16[64,20224]{1,0:T(8,128)(2,1)S(1)}, bf16[64,20224]{1,0:T(8,128)(2,1)}, u32[]{:S(2)}) copy-start(bf16[64,20224]{1,0:T(8,128)(2,1)} %param.11) | copy-start | bytes 7766020
  0.9 5.5 %copy-start.3 = (bf16[64,294]{1,0:T(8,128)(2,1)S(1)}, bf16[64,294]{1,0:T(8,128)(2,1)}, u32[]{:S(2)}) copy-start(bf16[64,294]{1,0:T(8,128)(2,1)} %param.10) | copy-start | bytes 112900
  47.3 8.2 %copy-start.1 = (s32[316,128]{1,0:T(8,128)S(1)}, s32[316,128]{1,0:T(8,128)}, u32[]{:S(2)}) copy-start(s32[316,128]{1,0:T(8,128)} %param.14) | copy-start | bytes 485380
  48.7 38.9 %all-to-all-start.1 = ((bf16[8,1088,64]{1,2,0:T(8,128)(2,1)}), bf16[8,1088,64]{1,2,0:T(8,128)(2,1)}, u32[]{:S(2)}, u32[]{:S(2)}) async-start(bf16[8,1088,64]{1,2,0:T(8,128)(2,1)} %broadcast_in_dim.10), calls=%async_computation.1 | async-start | bytes 2359296 | tf_op jit(solution)/shard_map/all_to_all | solution.py:15
  170.7 11.3 %copy-start.2 = (bf16[294,64]{0,1:T(8,128)(2,1)S(1)}, bf16[294,64]{0,1:T(8,128)(2,1)}, u32[]{:S(2)}) copy-start(bf16[294,64]{0,1:T(8,128)(2,1)} %param.12) | copy-start | bytes 112900
where the time goes:
time: 190 us
  local copies, waits for them, and re-layouts  107 us (56%)
  blocking collectives  34.5 us (18%)
  waiting for transfers between devices  31.3 us (16%)
  matrix products  9 us (5%)
  starting transfers between devices  6.82 us (4%)
    gather x1, local copies, waits for them, and re-layouts, on_device(): picked = extended[index].reshape(box_count, -1)  76.6 us
    all_to_all x1, blocking collectives, on_device(): lax.all_to_all(source, 'grp', split_axis=0, concat_axis=0, tiled=True)  34.5 us
    all_to_all x1, waiting for transfers between devices, from_everyone(): return lax.all_to_all(copies, axis, split_axis=0, concat_axis=0, tiled=True)  31.3 us
    reshape x1, local copies, waits for them, and re-layouts, on_device(): picked = extended[index].reshape(box_count, -1)  11.3 us
    unnamed x14, local copies, waits for them, and re-layouts  6.9 us
    all_to_all x1, starting transfers between devices, from_everyone(): return lax.all_to_all(copies, axis, split_axis=0, concat_axis=0, tiled=True)  6.82 us
    dot_general x1, matrix products, on_device(): lax.dot_general(expand_matrix, local_coeff, (((1,), (1,)), ((), ())), pre...  4.52 us
  transfers between devices with their start and end apart: 1, of which 1 were waited for; matrix products, arithmetic and copies ran while one was open for 0% of the time, Pallas kernels for 0%

commit v1 on v0

--- a/solution.py
+++ b/solution.py
@@ -1,9 +1,54 @@
+import functools
 import jax
 import jax.numpy as jnp
 from jax import lax
+from jax.experimental import pallas as pl
+from jax.experimental.pallas import tpu as pltpu
 from jax.sharding import PartitionSpec as P
 
+F32=jnp.float32; BF=jnp.bfloat16
+NT=(((1,),(1,)),((),()))
+def kb(idx_ref, pool_ref, t_ref, e_ref, d_ref, out_ref, taba, tabb, st0, st1, dsc, acc):
+    n = pool_ref.shape[0]
+    ch = 256
+    zero64 = jnp.zeros((ch,64),F32)
+    @pl.loop(0, n//ch)
+    def _(r):
+        rows = pl.ds(pl.multiple_of(r*ch,ch),ch)
+        x = pool_ref[rows,:].astype(F32)
+        taba[rows,:] = jnp.concatenate([x,zero64],axis=1)
+        tabb[rows,:] = jnp.concatenate([zero64,x],axis=1)
+    taba[pl.ds(n,8),:] = jnp.zeros((8,128),F32)
+    tabb[pl.ds(n,8),:] = jnp.zeros((8,128),F32)
+    acc[...] = jnp.zeros_like(acc)
+    pairs = idx_ref.shape[0]//4
+    def gather(kk, st):
+        for j in range(2):
+            o = 4*kk+2*j
+            for t in range(128):
+                st[j, pl.ds(t,1), :] = taba[pl.ds(idx_ref[o,t],1),:] + tabb[pl.ds(idx_ref[o+1,t],1),:]
+    @pl.loop(0, pairs)
+    def _(kk):
+        gather(kk, st0)
+        p = jnp.concatenate([st0[0],st0[1]],axis=1).astype(BF)
+        tt = t_ref[:, pl.ds(pl.multiple_of(kk*256,256),256)]
+        acc[...] += lax.dot_general(tt, p, NT, preferred_element_type=F32)
+    lc = acc[...].astype(BF)
+    lm = jnp.dot(e_ref[...], lc, preferred_element_type=F32).astype(BF)
+    ne = d_ref.shape[0]
+    d2 = d_ref[...].reshape(ne*8, ne)
+    dsc[...] = jnp.dot(d2, lm, preferred_element_type=F32)
+    for c in range(8):
+        out_ref[:, c*128:(c+1)*128] = dsc[pl.ds(c, ne, stride=8),:].astype(BF)
 
+def m2l(idx, pool, t, e, d):
+    ne = d.shape[0]
+    n = pool.shape[0]
+    V=pl.BlockSpec(memory_space=pltpu.VMEM)
+    return pl.pallas_call(kb, out_shape=jax.ShapeDtypeStruct((ne,1024),BF),
+      in_specs=[pl.BlockSpec(memory_space=pltpu.SMEM),V,V,V,V], out_specs=V,
+      scratch_shapes=[pltpu.VMEM((n+8,128),F32),pltpu.VMEM((n+8,128),F32),pltpu.VMEM((2,128,128),F32),pltpu.VMEM((2,128,128),F32),pltpu.VMEM((ne*8,128),F32),pltpu.VMEM((64,128),F32)],
+      compiler_params=pltpu.CompilerParams(vmem_limit_bytes=56*2**20))(idx,pool,t,e,d)
 def in_order(pieces, dim):
     pieces = jnp.moveaxis(pieces, 0, dim)
     shape = pieces.shape
@@ -50,30 +95,14 @@
     width = box_count + ghost_width
     group_boxes = sub_count * box_count
     pool_size = sub_count * width
-    lists = jnp.transpose(neighbour_list)
+    lists = neighbour_list
     ghost_index = lists - group_boxes
     own_place = lists // box_count * width + lists % box_count
     ghost_place = ghost_index // ghost_width * width + box_count + ghost_index % ghost_width
     remap = jnp.where(lists < group_boxes, own_place, ghost_place)
-    remap = jnp.where(lists < pool_size, remap, -1)
+    remap = jnp.where(lists < pool_size, remap, pool_size)
     whole_pool = gather_directly(mine, "sub", 0)
-    span = whole_pool.shape[0]
-    local = remap - 0
-    valid = (local >= 0) & (local < span)
-    index = jnp.where(valid, local, span)
-    extended = jnp.concatenate([whole_pool, jnp.zeros((1, coeff_rows), jnp.bfloat16)], axis=0)
-    picked = extended[index].reshape(box_count, -1)
-    local_float = lax.dot_general(
-        picked, transfer_matrix, (((1,), (1,)), ((), ())), preferred_element_type=jnp.float32
-    )
-    local_coeff = local_float.astype(jnp.bfloat16)
-    local_moment = lax.dot_general(
-        expand_matrix, local_coeff, (((1,), (1,)), ((), ())), preferred_element_type=jnp.float32
-    ).astype(jnp.bfloat16)
-    result = jnp.einsum(
-        "icj,jb->icb", downward_matrix, local_moment, preferred_element_type=jnp.float32
-    )
-    return result.reshape(surface, 8 * box_count).astype(jnp.bfloat16)
+    return m2l(remap, whole_pool, transfer_matrix, expand_matrix, downward_matrix)
 
 
 def solution(mesh):

time: 190 us -> 141 us (0.74)
  local copies, waits for them, and re-layouts: 107 us -> 12.6 us
  Pallas kernels: 0 us -> 54.2 us
  matrix products: 9 us -> 0.87 us
    gather x1 -> x0, local copies, waits for them, and re-layouts: 76.6 us -> none  [on_device(): picked = extended[index].reshape(box_count, -1)]
    pallas_call x0 -> x1, Pallas kernels: none -> 54.2 us  [m2l(): pl.pallas_call(kb, out_shape=jax.ShapeDtypeStruct((ne, 1024), BF), in_spe...]
    reshape x1 -> x0, local copies, waits for them, and re-layouts: 11.3 us -> none  [on_device(): picked = extended[index].reshape(box_count, -1)]
    dot_general x2 -> x0, matrix products: 6.65 us -> none  [the longest x1 4.52 us: on_device(): lax.dot_general(expand_matrix, local_coeff, (((1,), (1,)), ((), ())), pre...]
    concatenate x1 -> x0, local copies, waits for them, and re-layouts: 2.83 us -> none  [on_device(): jnp.concatenate([whole_pool, jnp.zeros((1, coeff_rows), jnp.bfloat16)], a...]
    unnamed x14 -> x15, local copies, waits for them, and re-layouts: 6.9 us -> 5.2 us
  transfers between devices with their start and end apart: 1 -> 1, of which waited for: 1 -> 1; matrix products, arithmetic and copies ran while one was open for 0% -> 1% of each run, Pallas kernels for 0% -> 0%
where the time goes in v1:
time: 141 us; the launch traced here: 140 us
  Pallas kernels  54.2 us (38%)
  blocking collectives  34.5 us (24%)
  waiting for transfers between devices  30.2 us (21%)
  local copies, waits for them, and re-layouts  12.6 us (9%)
  starting transfers between devices  6.82 us (5%)
    pallas_call x1, Pallas kernels, m2l(): pl.pallas_call(kb, out_shape=jax.ShapeDtypeStruct((ne, 1024), BF), in_spe...  54.2 us
    all_to_all x1, blocking collectives, on_device(): lax.all_to_all(source, 'grp', split_axis=0, concat_axis=0, tiled=True)  34.5 us
    all_to_all x1, waiting for transfers between devices, from_everyone(): return lax.all_to_all(copies, axis, split_axis=0, concat_axis=0, tiled=True)  30.2 us
    all_to_all x1, starting transfers between devices, from_everyone(): return lax.all_to_all(copies, axis, split_axis=0, concat_axis=0, tiled=True)  6.82 us
    unnamed x15, local copies, waits for them, and re-layouts  5.2 us
    gather x1, local copies, waits for them, and re-layouts, on_device(): jnp.concatenate([packed_rows, jnp.zeros((1, coeff_rows), jnp.bfloat16)],...  3.3 us
  transfers between devices with their start and end apart: 1, of which 1 were waited for; matrix products, arithmetic and copies ran while one was open for 1% of the time, Pallas kernels for 0%

profile of v1, /device:TPU:1, one launch (start us, length us, event | category | flops | bytes accessed | tf_op | source)
XLA Modules:
  0.0 140.5 jit_solution(1450179717732806382)
XLA Ops:
  0.0 0.0 copy-start
  0.0 0.0 copy-start.1
  0.0 3.9 %copy.15 = bf16[294,8,294]{0,1,2:T(8,128)(2,1)S(1)} copy(bf16[294,8,294]{2,1,0:T(8,128)(2,1)} %param.9) | data formatting | bytes 2765952 | tf_op args[1]
  3.9 0.0 copy-done.1
  3.9 0.1 copy.22
  4.0 0.0 copy-done
  4.0 0.0 copy-start.4
  4.0 0.9 fusion.2
  4.9 0.1 copy.17
  5.0 0.0 copy-done.4
  5.1 3.3 %gather_fusion = bf16[960,64]{1,0:T(8,128)(2,1)S(1)} fusion(bf16[129,64]{1,0:T(8,128)(2,1)S(1)} %concatenate.6.clone, s32[1024]{0:T(1024)S(1)} %pad_clamp_fusion), kind=kCustom, calls=%fused_computation | custom fusion | bytes 249600 | tf_op jit(solution)/shard_map/gather | solution.py:88
  8.4 0.1 all_to_all.11
  8.5 0.2 reshape.51
  8.7 34.5 %all_to_all.17 = bf16[96,2,320]{2,1,0:T(2,128)(2,1)S(1)} all-to-all(bf16[96,2,320]{2,1,0:T(2,128)(2,1)S(1)} %reshape.51), channel_id=1, replica_groups=mesh['grp'=96,'sub'=8] {'grp'}, dimensions={0} | all-to-all | bytes 245760 | tf_op jit(solution)/shard_map/all_to_all | solution.py:91
  43.2 0.2 reshape.52
  43.4 0.1 all_to_all.13
  43.6 0.1 pad_maximum_fusion
  43.6 0.2 copy.18
  43.8 0.0 copy-start.3
  43.8 0.0 copy-start.2
  43.8 1.2 broadcast_in_dim.4
  45.0 6.8 %all-to-all-start.1 = ((bf16[8,1088,64]{1,2,0:T(8,128)(2,1)}), bf16[8,1088,64]{1,2,0:T(8,128)(2,1)S(1)}, u32[]{:S(2)}, u32[]{:S(2)}) async-start(bf16[8,1088,64]{1,2,0:T(8,128)(2,1)} %broadcast_in_dim.4), calls=%async_computation.1 | async-start | bytes 2359296 | tf_op jit(solution)/shard_map/all_to_all | solution.py:60
  51.8 0.0 copy-done.3
  51.8 0.7 copy.20.e_ref
  52.5 0.0 copy-done.2
  52.6 1.0 fusion.8.idx_ref
  53.6 30.2 %all-to-all-done.1 = bf16[8,1088,64]{1,2,0:T(8,128)(2,1)S(1)} async-done(((bf16[8,1088,64]{1,2,0:T(8,128)(2,1)}), bf16[8,1088,64]{1,2,0:T(8,128)(2,1)S(1)}, u32[]{:S(2)}, u32[]{:S(2)}) %all-to-all-start.1) | async-done | bytes 1114144 | tf_op jit(solution)/shard_map/all_to_all | solution.py:60
  83.8 2.4 %copy.19 = bf16[8,1088,64]{2,1,0:T(8,128)(2,1)} copy(bf16[8,1088,64]{1,2,0:T(8,128)(2,1)S(1)} %all-to-all-done.1) | data formatting | bytes 2228224 | tf_op jit(solution)/shard_map/all_to_all | solution.py:60
  86.2 54.2 %shard_map.82 = bf16[294,1024]{1,0:T(8,128)(2,1)} custom-call(s32[316,128]{1,0:T(8,128)} %fusion.8.idx_ref, bf16[8704,64]{1,0:T(8,128)(2,1)} %bitcast.17, bf16[64,20224]{1,0:T(8,128)(2,1)} %t_ref.1, bf16[294,64]{1,0:T(8,128)(2,1)} %copy.20.e_ref, bf16[294,8,294]{2,1,0:T(8,128)(2,1)} %d_ref.1), custom_call_target="tpu_custom_call" | custom-call | tf_op jit(solution)/shard_map/pallas_call | solution.py:48
  (3 shorter events, 0.0 us)
Async XLA Ops:
  0.0 4.0 %copy-start = (bf16[64,294]{1,0:T(8,128)(2,1)S(1)}, bf16[64,294]{1,0:T(8,128)(2,1)}, u32[]{:S(2)}) copy-start(bf16[64,294]{1,0:T(8,128)(2,1)} %param.10) | copy-start | bytes 112900
  0.0 3.9 %copy-start.1 = (bf16[294,1024]{1,0:T(8,128)(2,1)S(1)}, bf16[294,1024]{1,0:T(8,128)(2,1)}, u32[]{:S(2)}) copy-start(bf16[294,1024]{1,0:T(8,128)(2,1)} %param.8) | copy-start | bytes 1806340
  4.0 1.0 copy-start.4
  43.8 8.0 %copy-start.3 = (bf16[294,64]{0,1:T(8,128)(2,1)S(1)}, bf16[294,64]{0,1:T(8,128)(2,1)}, u32[]{:S(2)}) copy-start(bf16[294,64]{0,1:T(8,128)(2,1)} %param.12) | copy-start | bytes 112900
  43.8 8.7 %copy-start.2 = (s32[316,128]{1,0:T(8,128)S(1)}, s32[316,128]{1,0:T(8,128)}, u32[]{:S(2)}) copy-start(s32[316,128]{1,0:T(8,128)} %param.14) | copy-start | bytes 485380
  45.0 38.8 %all-to-all-start.1 = ((bf16[8,1088,64]{1,2,0:T(8,128)(2,1)}), bf16[8,1088,64]{1,2,0:T(8,128)(2,1)S(1)}, u32[]{:S(2)}, u32[]{:S(2)}) async-start(bf16[8,1088,64]{1,2,0:T(8,128)(2,1)} %broadcast_in_dim.4), calls=%async_computation.1 | async-start | bytes 2359296 | tf_op jit(solution)/shard_map/all_to_all | solution.py:60

commit v2 on v0

v2 whole, which is shorter than its diff:
```python
import functools
import jax
import jax.numpy as jnp
from jax import lax
from jax.experimental import pallas as pl
from jax.experimental.pallas import tpu as pltpu

from jax.sharding import PartitionSpec as P

F32, BF, I32 = jnp.float32, jnp.bfloat16, jnp.int32
NT = (((1,), (1,)), ((), ()))
VM = pl.BlockSpec(memory_space=pltpu.VMEM)
GH_ROWS = 144


def exchange_kernel(n_grp, n_sub, gs_ref, gv_ref, x_ref, u_ref, p_ref, own_out, gh_out, rank_out,
                    uf, tab, sf, send, recv, own, ownr, comp, ghr, hot,
                    own_send, own_recv, slot_send, slot_recv, gh_send, gh_recv):
    me_g, me_s = lax.axis_index("grp"), lax.axis_index("sub")
    ne = u_ref.shape[0]
    barrier = pltpu.get_barrier_semaphore()

    def grp_peer(d):
        return lax.rem(me_g + d, n_grp)

    def sub_peer(d):
        return lax.rem(me_s + d, n_sub)

    @pl.loop(1, n_grp)
    def _(d):
        pl.semaphore_signal(barrier, inc=1, device_id={"grp": grp_peer(d), "sub": me_s},
                            device_id_type=pl.DeviceIdType.MESH)

    @pl.loop(1, n_sub)
    def _(d):
        pl.semaphore_signal(barrier, inc=1, device_id={"grp": me_g, "sub": sub_peer(d)},
                            device_id_type=pl.DeviceIdType.MESH)

    flat = u_ref[...].reshape(ne * 8, ne).astype(F32)
    starts = range(0, ne, 128)
    for n, at in enumerate(starts):
        width = min(128, ne - at)
        uf[n, :, pl.ds(0, width)] = flat[:, at : at + width]
    total = jnp.zeros((ne, 128), F32)
    for c in range(8):
        tiles = [uf[n, pl.ds(c, ne, stride=8), :].astype(BF) for n in range(len(starts))]
        tiles[-1] = tiles[-1][:, : ne - starts[-1]]
        total += jnp.dot(jnp.concatenate(tiles, axis=1), x_ref[:, c * 128 : (c + 1) * 128],
                         preferred_element_type=F32)
    parent = total.astype(BF)
    twice = jnp.concatenate([p_ref[...], p_ref[...]], axis=0)
    packed = jnp.dot(twice, parent, preferred_element_type=F32).T.astype(BF).astype(F32)
    lo64 = lax.broadcasted_iota(I32, (1, 128), 1) < 64
    tab[pl.ds(0, 128), :] = packed
    tab[pl.ds(128, 8), :] = jnp.zeros((8, 128), F32)
    mine = jnp.where(lo64, packed[0:64], packed[64:128]).astype(BF)
    own[...] = mine
    ownr[me_s] = mine
    sf[...] = jnp.zeros_like(sf)

    @pl.loop(0, n_grp)
    def _(g):
        for k in range(5):
            sf[g, pl.ds(k, 1), :] = jnp.where(lo64, tab[pl.ds(gs_ref[0, g * 10 + k], 1), :],
                                              tab[pl.ds(gs_ref[0, g * 10 + 5 + k], 1), :])

    send[...] = sf[...].astype(BF)
    recv[me_g] = send[me_g]
    pl.semaphore_wait(barrier, n_grp + n_sub - 2)

    def own_copy(d):
        return pltpu.make_async_remote_copy(
            src_ref=own, dst_ref=ownr.at[me_s], send_sem=own_send, recv_sem=own_recv,
            device_id={"grp": me_g, "sub": sub_peer(d)}, device_id_type=pl.DeviceIdType.MESH)

    def slot_copy(d):
        g = grp_peer(d)
        return pltpu.make_async_remote_copy(
            src_ref=send.at[g], dst_ref=recv.at[me_g], send_sem=slot_send, recv_sem=slot_recv,
            device_id={"grp": g, "sub": me_s}, device_id_type=pl.DeviceIdType.MESH)

    def gh_copy(d):
        return pltpu.make_async_remote_copy(
            src_ref=comp, dst_ref=ghr.at[me_s], send_sem=gh_send, recv_sem=gh_recv,
            device_id={"grp": me_g, "sub": sub_peer(d)}, device_id_type=pl.DeviceIdType.MESH)

    @pl.loop(1, n_grp)
    def _(d):
        slot_copy(d).start()

    @pl.loop(1, n_sub)
    def _(d):
        own_copy(d).start()

    def iota(shape, dim):
        return lax.broadcasted_iota(I32, shape, dim)

    named = jnp.where(gv_ref[...] < 128, 1.0, 0.0)
    named = jnp.broadcast_to(named, (8, n_grp * 10)).astype(BF)
    slots = (n_grp * 10, 128)
    first = jnp.where(iota(slots, 0) == 10 * iota(slots, 1), 1.0, 0.0).astype(BF)
    near = jnp.dot(named, first, preferred_element_type=F32)
    square = (128, 128)
    below = jnp.where(iota(square, 0) < iota(square, 1), 1.0, 0.0).astype(BF)
    rank = jnp.dot(near.astype(BF), below, preferred_element_type=F32)
    rank_out[...] = rank.astype(I32)
    value = ((rank + 1.0) * near).astype(BF)
    wide = (128, n_grp * 8)
    copies = jnp.where(iota(wide, 0) == (iota(wide, 1) >> 3), 1.0, 0.0).astype(BF)
    value = jnp.dot(value, copies, preferred_element_type=F32)[0:1]
    k = iota((1, n_grp * 8), 1) & 7
    place = jnp.where((k < 5) & (value > 0.5), (value - 1.0) * 5.0 + k.astype(F32), -1.0)
    rows = iota((GH_ROWS, n_grp * 8), 0).astype(F32)
    hot[...] = jnp.where(rows == place, 1.0, 0.0).astype(BF)

    def all_slots(ref):
        return ref.at[pl.ds(0, n_grp - 1)]

    every_slot = pltpu.make_async_remote_copy(
        src_ref=all_slots(send), dst_ref=all_slots(recv), send_sem=slot_send, recv_sem=slot_recv,
        device_id={"grp": grp_peer(1), "sub": me_s}, device_id_type=pl.DeviceIdType.MESH)
    every_slot.wait_recv()
    got = recv[...].astype(F32).reshape(n_grp * 8, 128).astype(BF)
    packed_ghosts = jnp.dot(hot[...], got, preferred_element_type=F32).astype(BF)
    comp[...] = packed_ghosts
    ghr[me_s] = packed_ghosts

    @pl.loop(1, n_sub)
    def _(d):
        gh_copy(d).start()

    def every(ref, src, s_sem, r_sem):
        part = ref.at[pl.ds(0, n_sub - 1)]
        return pltpu.make_async_remote_copy(
            src_ref=part, dst_ref=part, send_sem=s_sem, recv_sem=r_sem,
            device_id={"grp": me_g, "sub": sub_peer(1)}, device_id_type=pl.DeviceIdType.MESH)

    every_own = every(ownr, own, own_send, own_recv)
    every_own.wait_recv()
    own_out[...] = ownr[...]
    every_slot.wait_send()
    every_own.wait_send()
    every_gh = every(ghr, comp, gh_send, gh_recv)
    every_gh.wait_recv()
    gh_out[...] = ghr[...]
    every_gh.wait_send()


def exchange(ghost_map, x, u, p, n_grp, n_sub):
    ne = u.shape[0]
    dma = pltpu.SemaphoreType.DMA
    return pl.pallas_call(
        functools.partial(exchange_kernel, n_grp, n_sub),
        out_shape=(
            jax.ShapeDtypeStruct((n_sub, 64, 128), BF),
            jax.ShapeDtypeStruct((n_sub, GH_ROWS, 128), BF),
            jax.ShapeDtypeStruct((8, 128), I32),
        ),
        in_specs=[pl.BlockSpec(memory_space=pltpu.SMEM)] + [VM] * 4,
        out_specs=(VM, VM, VM),
        scratch_shapes=[
            pltpu.VMEM((pl.cdiv(ne, 128), ne * 8, 128), F32),
            pltpu.VMEM((136, 128), F32),
            pltpu.VMEM((n_grp, 8, 128), F32),
            pltpu.VMEM((n_grp, 8, 128), BF),
            pltpu.VMEM((n_grp, 8, 128), BF),
            pltpu.VMEM((64, 128), BF),
            pltpu.VMEM((n_sub, 64, 128), BF),
            pltpu.VMEM((GH_ROWS, 128), BF),
            pltpu.VMEM((n_sub, GH_ROWS, 128), BF),
            pltpu.VMEM((GH_ROWS, n_grp * 8), BF),
        ] + [dma] * 6,
        compiler_params=pltpu.CompilerParams(
            collective_id=0, has_side_effects=True, vmem_limit_bytes=24 * 2**20),
    )(ghost_map, ghost_map, x, u, p)

BUF = 3


def m2l_kernel(nbr_ref, rank_ref, own_ref, gh_ref, t_ref, e_ref, d_ref, out_ref,
               tab, idxv, sem, acc, dsc, *bufs):
    sms, sts = bufs[:BUF], bufs[BUF:]
    offs = nbr_ref.shape[0]
    full = offs // 8
    tail = offs - 8 * full
    zero_row = 1024 + 16 * GH_ROWS
    ranks = rank_ref[...]

    def place(v):
        rank = ranks[: v.shape[0]]
        w = jnp.maximum(v - 1024, 0)
        s = (w * 8739) >> 23
        u = w - s * 960
        g = (u * 6554) >> 16
        k = u - g * 10
        r = jnp.take_along_axis(rank, g, axis=1)
        half = jnp.where(k >= 5, 1, 0)
        row = 1024 + s * (2 * GH_ROWS) + half * GH_ROWS + r * 5 + (k - 5 * half)
        row = jnp.where(v < 1024, v, row)
        return jnp.where(v >= 8704, zero_row, row)

    idxv[pl.ds(0, 8), :] = jnp.concatenate(
        [place(nbr_ref[pl.ds(0, tail), :]), jnp.full((8 - tail, 128), zero_row, I32)], axis=0)
    for i in range(full):
        idxv[pl.ds(8 * i + 8, 8), :] = place(nbr_ref[pl.ds(tail + 8 * i, 8), :])

    def fetch(i, b):
        return pltpu.make_async_copy(idxv.at[pl.ds(pl.multiple_of(i * 8, 8), 8)], sms[b], sem.at[b])

    for b in range(BUF):
        fetch(b, b).start()
    lo64 = lax.broadcasted_iota(I32, (1, 128), 1) < 64

    def spread(src, base, rows):
        x = src.astype(F32)
        y = pltpu.roll(x, 64, 1)
        tab[pl.ds(pl.multiple_of(base, 8), rows), :] = jnp.where(lo64, x, y)
        tab[pl.ds(pl.multiple_of(base + rows, 8), rows), :] = jnp.where(lo64, y, x)

    for s in range(8):
        spread(own_ref[s], s * 128, 64)
        spread(gh_ref[s], 1024 + s * 2 * GH_ROWS, GH_ROWS)
    tab[pl.ds(zero_row, 8), :] = jnp.zeros((8, 128), F32)
    acc[...] = jnp.zeros_like(acc)

    def gather(sm, st, rows):
        for o in range(0, rows, 2):
            for t in range(128):
                st[o // 2, pl.ds(t, 1), :] = jnp.where(
                    lo64, tab[pl.ds(sm[o, t], 1), :], tab[pl.ds(sm[o + 1, t], 1), :])

    def product(first, st, rows):
        p = jnp.concatenate([st[j] for j in range(rows // 2)], axis=1).astype(BF)
        tt = t_ref[:, pl.ds(pl.multiple_of(first * 64, 256), rows * 64)]
        acc[...] += lax.dot_general(tt, p, NT, preferred_element_type=F32)

    fetch(0, 0).wait()
    gather(sms[0], sts[0], tail)
    product(0, sts[0], tail)
    fetch(BUF, 0).start()

    @pl.loop(0, full // BUF)
    def _(j):
        for c in range(BUF):
            b = (c + 1) % BUF
            i = BUF * j + c
            fetch(i + 1, b).wait()
            gather(sms[b], sts[b], 8)
            product(tail + 8 * i, sts[b], 8)

            @pl.when(i + 1 + BUF <= full)
            def _():
                fetch(i + 1 + BUF, b).start()

    lc = acc[...].astype(BF)
    lm = jnp.dot(e_ref[...], lc, preferred_element_type=F32).astype(BF)
    ne = d_ref.shape[0]
    dsc[...] = jnp.dot(d_ref[...].reshape(ne * 8, ne), lm, preferred_element_type=F32)
    for c in range(8):
        out_ref[:, c * 128 : (c + 1) * 128] = dsc[pl.ds(c, ne, stride=8), :].astype(BF)


def m2l(nbr, rank, own, gh, t, e, d):
    ne = d.shape[0]
    return pl.pallas_call(
        m2l_kernel,
        out_shape=jax.ShapeDtypeStruct((ne, 1024), BF),
        in_specs=[VM] * 7,
        out_specs=VM,
        scratch_shapes=[
            pltpu.VMEM((1024 + 16 * GH_ROWS + 8, 128), F32),
            pltpu.VMEM((320, 128), I32),
            pltpu.SemaphoreType.DMA((BUF,)),
            pltpu.VMEM((64, 128), F32),
            pltpu.VMEM((ne * 8, 128), F32),
            *[pltpu.SMEM((8, 128), I32)] * BUF,
            *[pltpu.VMEM((4, 128, 128), F32)] * BUF,
        ],
        compiler_params=pltpu.CompilerParams(vmem_limit_bytes=24 * 2**20),
    )(nbr, rank, own, gh, t, e, d)


def on_device(
    child_moments,
    upward_matrix,
    project_matrix,
    transfer_matrix,
    expand_matrix,
    downward_matrix,
    neighbour_list,
    ghost_map,
):
    own, ghosts, ranks = exchange(ghost_map, child_moments, upward_matrix, project_matrix,
                                  lax.axis_size("grp"), lax.axis_size("sub"))
    return m2l(neighbour_list, ranks, own, ghosts, transfer_matrix, expand_matrix, downward_matrix)


def solution(mesh):
    return jax.shard_map(
        on_device,
        mesh=mesh,
        in_specs=(
            P(None, ("grp", "sub")),
            P(),
            P(),
            P(),
            P(),
            P(),
            P(None, ("grp", "sub")),
            P(("grp", "sub"), None),
        ),
        out_specs=P(None, ("grp", "sub")),
        check_vma=False,
    )
```

time: 190 us -> 78.3 us (0.41)
  local copies, waits for them, and re-layouts: 107 us -> 7.51 us
  Pallas kernels: 0 us -> 70.4 us
  blocking collectives: 34.5 us -> 0 us
  waiting for transfers between devices: 31.3 us -> 0 us
  matrix products: 9 us -> 0 us
  starting transfers between devices: 6.82 us -> 0 us
    gather x2 -> x0, local copies, waits for them, and re-layouts: 79.9 us -> none  [the longest x1 76.6 us: on_device(): picked = extended[index].reshape(box_count, -1)]
    pallas_call x0 -> x2, Pallas kernels: none -> 70.4 us  [the longest x1 41.9 us: exchange(): pl.pallas_call(functools.partial(exchange_kernel, n_grp, n_sub), out_shap...]
    all_to_all x1 -> x0, blocking collectives: 34.5 us -> none  [on_device(): lax.all_to_all(source, 'grp', split_axis=0, concat_axis=0, tiled=True)]
    all_to_all x1 -> x0, waiting for transfers between devices: 31.3 us -> none  [from_everyone(): return lax.all_to_all(copies, axis, split_axis=0, concat_axis=0, tiled=True)]
    reshape x1 -> x0, local copies, waits for them, and re-layouts: 11.3 us -> none  [on_device(): picked = extended[index].reshape(box_count, -1)]
    dot_general x3 -> x0, matrix products: 9 us -> none  [the longest x1 4.52 us: on_device(): lax.dot_general(expand_matrix, local_coeff, (((1,), (1,)), ((), ())), pre...]
    all_to_all x1 -> x0, starting transfers between devices: 6.82 us -> none  [from_everyone(): return lax.all_to_all(copies, axis, split_axis=0, concat_axis=0, tiled=True)]
    all_to_all x3 -> x0, local copies, waits for them, and re-layouts: 3.91 us -> none  [the longest x1 3.68 us: from_everyone(): return lax.all_to_all(copies, axis, split_axis=0, concat_axis=0, tiled=True)]
  transfers between devices with their start and end apart: 1 -> 0, of which waited for: 1 -> 0; matrix products, arithmetic and copies ran while one was open for 0% -> 0% of each run, Pallas kernels for 0% -> 0%
where the time goes in v2:
time: 78.3 us; the launch traced here: 77.9 us
  Pallas kernels  70.4 us (90%)
  local copies, waits for them, and re-layouts  7.51 us (10%)
    pallas_call x1, Pallas kernels, exchange(): pl.pallas_call(functools.partial(exchange_kernel, n_grp, n_sub), out_shap...  41.9 us
    pallas_call x1, Pallas kernels, m2l(): pl.pallas_call(m2l_kernel, out_shape=jax.ShapeDtypeStruct((ne, 1024), BF)...  28.5 us
    unnamed x15, local copies, waits for them, and re-layouts  7.51 us

profile of v2, /device:TPU:1, one launch (start us, length us, event | category | flops | bytes accessed | tf_op | source)
XLA Modules:
  0.0 77.9 jit_solution(17388561515058243081)
XLA Ops:
  0.0 0.0 copy-start
  0.0 1.1 %copy.9.e_ref = bf16[294,64]{1,0:T(8,128)(2,1)S(1)} copy(bf16[294,64]{0,1:T(8,128)(2,1)} %param.12) | data formatting | bytes 75264 | tf_op args[4]
  1.1 0.0 copy-start.2
  1.1 1.5 %copy-done.2 = bf16[294,8,294]{2,1,0:T(8,128)(2,1)S(1)} copy-done((bf16[294,8,294]{2,1,0:T(8,128)(2,1)S(1)}, bf16[294,8,294]{2,1,0:T(8,128)(2,1)}, u32[]{:S(2)}) %copy-start.2) | copy-done | bytes 1383000
  2.6 0.0 copy-start.3
  2.6 1.1 %copy-done.3 = bf16[294,1024]{1,0:T(8,128)(2,1)S(1)} copy-done((bf16[294,1024]{1,0:T(8,128)(2,1)S(1)}, bf16[294,1024]{1,0:T(8,128)(2,1)}, u32[]{:S(2)}) %copy-start.3) | copy-done | bytes 602136
  3.6 0.0 copy-start.5
  3.6 0.8 %copy-done.5 = bf16[64,294]{1,0:T(8,128)(2,1)S(1)} copy-done((bf16[64,294]{1,0:T(8,128)(2,1)S(1)}, bf16[64,294]{1,0:T(8,128)(2,1)}, u32[]{:S(2)}) %copy-start.5) | copy-done | bytes 37656
  4.4 0.0 copy-start.6
  4.4 0.7 copy-done.6
  5.1 41.9 %shard_map.82 = (bf16[8,64,128]{2,1,0:T(8,128)(2,1)S(1)}, bf16[8,144,128]{2,1,0:T(8,128)(2,1)S(1)}, s32[8,128]{1,0:T(8,128)S(1)}) custom-call(s32[1,960]{1,0:T(1,128)S(1)} %copy-done.6, s32[1,960]{1,0:T(1,128)S(1)} %copy-done.6, bf16[294,1024]{1,0:T(8,128)(2,1)S(1)} %copy-done.3, bf16[294,8,294]{2,1,0:T(8,128)(2,1)S(1)} %copy-done.2, ...), custom_call_target="tpu_custom_call" | custom-call | tf_op jit(solution)/shard_map/pallas_call | solution.py:152
  47.0 0.0 copy-done
  47.0 0.0 copy-start.1
  47.1 1.5 %copy-done.1 = bf16[294,8,294]{2,1,0:T(8,128)(2,1)S(1)} copy-done((bf16[294,8,294]{2,1,0:T(8,128)(2,1)S(1)}, bf16[294,8,294]{2,1,0:T(8,128)(2,1)}, u32[]{:S(2)}) %copy-start.1) | copy-done | bytes 1383000
  48.5 0.0 copy-start.4
  48.5 0.9 %copy-done.4 = s32[316,128]{1,0:T(8,128)S(1)} copy-done((s32[316,128]{1,0:T(8,128)S(1)}, s32[316,128]{1,0:T(8,128)}, u32[]{:S(2)}) %copy-start.4) | copy-done | bytes 161816
  49.4 28.5 %shard_map.83 = bf16[294,1024]{1,0:T(8,128)(2,1)} custom-call(s32[316,128]{1,0:T(8,128)S(1)} %copy-done.4, s32[8,128]{1,0:T(8,128)S(1)} %get-tuple-element.8.rank_ref, bf16[8,64,128]{2,1,0:T(8,128)(2,1)S(1)} %get-tuple-element.9.own_ref, bf16[8,144,128]{2,1,0:T(8,128)(2,1)S(1)} %get-tuple-element.10.gh_ref, bf16[64,20224]{1,0:T(8,128)(2,1)S(1)} %copy-done, ...), custom_call_target="tpu_custom_call" | custom-call | tf_op jit(solution)/shard_map/pallas_call | solution.py:265
Async XLA Ops:
  0.0 47.0 %copy-start = (bf16[64,20224]{1,0:T(8,128)(2,1)S(1)}, bf16[64,20224]{1,0:T(8,128)(2,1)}, u32[]{:S(2)}) copy-start(bf16[64,20224]{1,0:T(8,128)(2,1)} %t_ref.1) | copy-start | bytes 7766020
  1.1 1.5 %copy-start.2 = (bf16[294,8,294]{2,1,0:T(8,128)(2,1)S(1)}, bf16[294,8,294]{2,1,0:T(8,128)(2,1)}, u32[]{:S(2)}) copy-start(bf16[294,8,294]{2,1,0:T(8,128)(2,1)} %u_ref.1) | copy-start | bytes 4148932
  2.6 1.1 %copy-start.3 = (bf16[294,1024]{1,0:T(8,128)(2,1)S(1)}, bf16[294,1024]{1,0:T(8,128)(2,1)}, u32[]{:S(2)}) copy-start(bf16[294,1024]{1,0:T(8,128)(2,1)} %x_ref.1) | copy-start | bytes 1806340
  3.6 0.8 %copy-start.5 = (bf16[64,294]{1,0:T(8,128)(2,1)S(1)}, bf16[64,294]{1,0:T(8,128)(2,1)}, u32[]{:S(2)}) copy-start(bf16[64,294]{1,0:T(8,128)(2,1)} %p_ref.1) | copy-start | bytes 112900
  4.4 0.7 copy-start.6
  47.0 1.5 %copy-start.1 = (bf16[294,8,294]{2,1,0:T(8,128)(2,1)S(1)}, bf16[294,8,294]{2,1,0:T(8,128)(2,1)}, u32[]{:S(2)}) copy-start(bf16[294,8,294]{2,1,0:T(8,128)(2,1)} %d_ref.1) | copy-start | bytes 4148932
  48.5 0.9 %copy-start.4 = (s32[316,128]{1,0:T(8,128)S(1)}, s32[316,128]{1,0:T(8,128)}, u32[]{:S(2)}) copy-start(s32[316,128]{1,0:T(8,128)} %nbr_ref.1) | copy-start | bytes 485380

commit v3 on v2

--- a/solution.py
+++ b/solution.py
@@ -10,11 +10,27 @@
 F32, BF, I32 = jnp.float32, jnp.bfloat16, jnp.int32
 NT = (((1,), (1,)), ((), ()))
 VM = pl.BlockSpec(memory_space=pltpu.VMEM)
-GH_ROWS = 144
-
-
-def exchange_kernel(n_grp, n_sub, gs_ref, gv_ref, x_ref, u_ref, p_ref, own_out, gh_out, rank_out,
-                    uf, tab, sf, send, recv, own, ownr, comp, ghr, hot,
+HB = pl.BlockSpec(memory_space=pltpu.HBM)
+GH_ROWS = 136
+ZERO_ROW = 1024 + 16 * GH_ROWS
+
+
+def place(v, rank):
+    rank = rank[: v.shape[0]]
+    w = jnp.maximum(v - 1024, 0)
+    s = (w * 8739) >> 23
+    u = w - s * 960
+    g = (u * 6554) >> 16
+    k = u - g * 10
+    r = jnp.take_along_axis(rank, g, axis=1)
+    half = jnp.where(k >= 5, 1, 0)
+    row = 1024 + s * (2 * GH_ROWS) + half * GH_ROWS + r * 5 + (k - 5 * half)
+    row = jnp.where(v < 1024, v, row)
+    return jnp.where(v >= 8704, ZERO_ROW, row)
+
+
+def exchange_kernel(n_grp, n_sub, g_hbm, x_hbm, u_hbm, p_hbm, n_hbm, own_out, gh_out, idx_out,
+                    gs_ref, gv_ref, x_ref, u_ref, p_ref, nbr_ref, in_sem, uf, tab, sf, send, recv, own, ownr, comp, ghr, hot,
                     own_send, own_recv, slot_send, slot_recv, gh_send, gh_recv):
     me_g, me_s = lax.axis_index("grp"), lax.axis_index("sub")
     ne = u_ref.shape[0]
@@ -36,11 +52,21 @@
         pl.semaphore_signal(barrier, inc=1, device_id={"grp": me_g, "sub": sub_peer(d)},
                             device_id_type=pl.DeviceIdType.MESH)
 
+    loads = [
+        pltpu.make_async_copy(src, dst, in_sem.at[n])
+        for n, (src, dst) in enumerate([(u_hbm, u_ref), (x_hbm, x_ref), (g_hbm, gs_ref),
+                                        (p_hbm, p_ref), (g_hbm, gv_ref), (n_hbm, nbr_ref)])
+    ]
+    for load in loads:
+        load.start()
+    loads[0].wait()
     flat = u_ref[...].reshape(ne * 8, ne).astype(F32)
     starts = range(0, ne, 128)
     for n, at in enumerate(starts):
         width = min(128, ne - at)
         uf[n, :, pl.ds(0, width)] = flat[:, at : at + width]
+    loads[1].wait()
+    loads[3].wait()
     total = jnp.zeros((ne, 128), F32)
     for c in range(8):
         tiles = [uf[n, pl.ds(c, ne, stride=8), :].astype(BF) for n in range(len(starts))]
@@ -57,6 +83,7 @@
     own[...] = mine
     ownr[me_s] = mine
     sf[...] = jnp.zeros_like(sf)
+    loads[2].wait()
 
     @pl.loop(0, n_grp)
     def _(g):
@@ -95,6 +122,7 @@
     def iota(shape, dim):
         return lax.broadcasted_iota(I32, shape, dim)
 
+    loads[4].wait()
     named = jnp.where(gv_ref[...] < 128, 1.0, 0.0)
     named = jnp.broadcast_to(named, (8, n_grp * 10)).astype(BF)
     slots = (n_grp * 10, 128)
@@ -103,15 +131,23 @@
     square = (128, 128)
     below = jnp.where(iota(square, 0) < iota(square, 1), 1.0, 0.0).astype(BF)
     rank = jnp.dot(near.astype(BF), below, preferred_element_type=F32)
-    rank_out[...] = rank.astype(I32)
+    ranks = rank.astype(I32)
     value = ((rank + 1.0) * near).astype(BF)
     wide = (128, n_grp * 8)
     copies = jnp.where(iota(wide, 0) == (iota(wide, 1) >> 3), 1.0, 0.0).astype(BF)
     value = jnp.dot(value, copies, preferred_element_type=F32)[0:1]
     k = iota((1, n_grp * 8), 1) & 7
-    place = jnp.where((k < 5) & (value > 0.5), (value - 1.0) * 5.0 + k.astype(F32), -1.0)
+    target = jnp.where((k < 5) & (value > 0.5), (value - 1.0) * 5.0 + k.astype(F32), -1.0)
     rows = iota((GH_ROWS, n_grp * 8), 0).astype(F32)
-    hot[...] = jnp.where(rows == place, 1.0, 0.0).astype(BF)
+    hot[...] = jnp.where(rows == target, 1.0, 0.0).astype(BF)
+
+    loads[5].wait()
+    offs = nbr_ref.shape[0]
+    tail = offs % 8
+    idx_out[pl.ds(0, 8), :] = jnp.concatenate(
+        [place(nbr_ref[pl.ds(0, tail), :], ranks), jnp.full((8 - tail, 128), ZERO_ROW, I32)], axis=0)
+    for i in range(offs // 8):
+        idx_out[pl.ds(8 * i + 8, 8), :] = place(nbr_ref[pl.ds(tail + 8 * i, 8), :], ranks)
 
     def all_slots(ref):
         return ref.at[pl.ds(0, n_grp - 1)]
@@ -146,7 +182,7 @@
     every_gh.wait_send()
 
 
-def exchange(ghost_map, x, u, p, n_grp, n_sub):
+def exchange(ghost_map, x, u, p, nbr, n_grp, n_sub):
     ne = u.shape[0]
     dma = pltpu.SemaphoreType.DMA
     return pl.pallas_call(
@@ -154,11 +190,18 @@
         out_shape=(
             jax.ShapeDtypeStruct((n_sub, 64, 128), BF),
             jax.ShapeDtypeStruct((n_sub, GH_ROWS, 128), BF),
-            jax.ShapeDtypeStruct((8, 128), I32),
+            jax.ShapeDtypeStruct((320, 128), I32),
         ),
-        in_specs=[pl.BlockSpec(memory_space=pltpu.SMEM)] + [VM] * 4,
+        in_specs=[HB] * 5,
         out_specs=(VM, VM, VM),
         scratch_shapes=[
+            pltpu.SMEM(ghost_map.shape, I32),
+            pltpu.VMEM(ghost_map.shape, I32),
+            pltpu.VMEM(x.shape, BF),
+            pltpu.VMEM(u.shape, BF),
+            pltpu.VMEM(p.shape, BF),
+            pltpu.VMEM(nbr.shape, I32),
+            dma((6,)),
             pltpu.VMEM((pl.cdiv(ne, 128), ne * 8, 128), F32),
             pltpu.VMEM((136, 128), F32),
             pltpu.VMEM((n_grp, 8, 128), F32),
@@ -172,40 +215,23 @@
         ] + [dma] * 6,
         compiler_params=pltpu.CompilerParams(
             collective_id=0, has_side_effects=True, vmem_limit_bytes=24 * 2**20),
-    )(ghost_map, ghost_map, x, u, p)
+    )(*[pltpu.with_memory_space_constraint(a, pltpu.HBM) for a in (ghost_map, x, u, p, nbr)])
 
 BUF = 3
 
 
-def m2l_kernel(nbr_ref, rank_ref, own_ref, gh_ref, t_ref, e_ref, d_ref, out_ref,
-               tab, idxv, sem, acc, dsc, *bufs):
+def m2l_kernel(idx_ref, own_ref, gh_ref, t_ref, e_hbm, d_hbm, out_ref,
+               tab, e_ref, d_ref, late_sem, sem, acc, dsc, *bufs):
     sms, sts = bufs[:BUF], bufs[BUF:]
-    offs = nbr_ref.shape[0]
-    full = offs // 8
-    tail = offs - 8 * full
-    zero_row = 1024 + 16 * GH_ROWS
-    ranks = rank_ref[...]
-
-    def place(v):
-        rank = ranks[: v.shape[0]]
-        w = jnp.maximum(v - 1024, 0)
-        s = (w * 8739) >> 23
-        u = w - s * 960
-        g = (u * 6554) >> 16
-        k = u - g * 10
-        r = jnp.take_along_axis(rank, g, axis=1)
-        half = jnp.where(k >= 5, 1, 0)
-        row = 1024 + s * (2 * GH_ROWS) + half * GH_ROWS + r * 5 + (k - 5 * half)
-        row = jnp.where(v < 1024, v, row)
-        return jnp.where(v >= 8704, zero_row, row)
-
-    idxv[pl.ds(0, 8), :] = jnp.concatenate(
-        [place(nbr_ref[pl.ds(0, tail), :]), jnp.full((8 - tail, 128), zero_row, I32)], axis=0)
-    for i in range(full):
-        idxv[pl.ds(8 * i + 8, 8), :] = place(nbr_ref[pl.ds(tail + 8 * i, 8), :])
+    full = idx_ref.shape[0] // 8 - 1
+    tail = t_ref.shape[1] // 64 - 8 * full
+    e_load = pltpu.make_async_copy(e_hbm, e_ref, late_sem.at[0])
+    d_load = pltpu.make_async_copy(d_hbm, d_ref, late_sem.at[1])
+    e_load.start()
+    d_load.start()
 
     def fetch(i, b):
-        return pltpu.make_async_copy(idxv.at[pl.ds(pl.multiple_of(i * 8, 8), 8)], sms[b], sem.at[b])
+        return pltpu.make_async_copy(idx_ref.at[pl.ds(pl.multiple_of(i * 8, 8), 8)], sms[b], sem.at[b])
 
     for b in range(BUF):
         fetch(b, b).start()
@@ -220,7 +246,7 @@
     for s in range(8):
         spread(own_ref[s], s * 128, 64)
         spread(gh_ref[s], 1024 + s * 2 * GH_ROWS, GH_ROWS)
-    tab[pl.ds(zero_row, 8), :] = jnp.zeros((8, 128), F32)
+    tab[pl.ds(ZERO_ROW, 8), :] = jnp.zeros((8, 128), F32)
     acc[...] = jnp.zeros_like(acc)
 
     def gather(sm, st, rows):
@@ -253,23 +279,27 @@
                 fetch(i + 1 + BUF, b).start()
 
     lc = acc[...].astype(BF)
-    lm = jnp.dot(e_ref[...], lc, preferred_element_type=F32).astype(BF)
+    e_load.wait()
+    lm = lax.dot_general(e_ref[...], lc, (((0,), (0,)), ((), ())), preferred_element_type=F32).astype(BF)
+    d_load.wait()
     ne = d_ref.shape[0]
     dsc[...] = jnp.dot(d_ref[...].reshape(ne * 8, ne), lm, preferred_element_type=F32)
     for c in range(8):
         out_ref[:, c * 128 : (c + 1) * 128] = dsc[pl.ds(c, ne, stride=8), :].astype(BF)
 
 
-def m2l(nbr, rank, own, gh, t, e, d):
+def m2l(idx, own, gh, t, e, d):
     ne = d.shape[0]
     return pl.pallas_call(
         m2l_kernel,
         out_shape=jax.ShapeDtypeStruct((ne, 1024), BF),
-        in_specs=[VM] * 7,
+        in_specs=[pl.BlockSpec(memory_space=pl.ANY)] + [VM] * 3 + [HB] * 2,
         out_specs=VM,
         scratch_shapes=[
             pltpu.VMEM((1024 + 16 * GH_ROWS + 8, 128), F32),
-            pltpu.VMEM((320, 128), I32),
+            pltpu.VMEM(e.shape[::-1], BF),
+            pltpu.VMEM(d.shape, BF),
+            pltpu.SemaphoreType.DMA((2,)),
             pltpu.SemaphoreType.DMA((BUF,)),
             pltpu.VMEM((64, 128), F32),
             pltpu.VMEM((ne * 8, 128), F32),
@@ -277,7 +307,7 @@
             *[pltpu.VMEM((4, 128, 128), F32)] * BUF,
         ],
         compiler_params=pltpu.CompilerParams(vmem_limit_bytes=24 * 2**20),
-    )(nbr, rank, own, gh, t, e, d)
+    )(idx, own, gh, t, *[pltpu.with_memory_space_constraint(a, pltpu.HBM) for a in (e.T, d)])
 
 
 def on_device(
@@ -290,9 +320,9 @@
     neighbour_list,
     ghost_map,
 ):
-    own, ghosts, ranks = exchange(ghost_map, child_moments, upward_matrix, project_matrix,
-                                  lax.axis_size("grp"), lax.axis_size("sub"))
-    return m2l(neighbour_list, ranks, own, ghosts, transfer_matrix, expand_matrix, downward_matrix)
+    own, ghosts, index = exchange(ghost_map, child_moments, upward_matrix, project_matrix,
+                                  neighbour_list, lax.axis_size("grp"), lax.axis_size("sub"))
+    return m2l(index, own, ghosts, transfer_matrix, expand_matrix, downward_matrix)
 
 
 def solution(mesh):

time: 78.3 us -> 70.2 us (0.90)
  local copies, waits for them, and re-layouts: 7.51 us -> 0.01 us
    unnamed x15 -> x2, local copies, waits for them, and re-layouts: 7.51 us -> 0.01 us
where the time goes in v3:
time: 70.2 us; the launch traced here: 69.7 us
  Pallas kernels  69.7 us (99%)
    pallas_call x1, Pallas kernels, exchange(): pl.pallas_call(functools.partial(exchange_kernel, n_grp, n_sub), out_shap...  41.3 us
    pallas_call x1, Pallas kernels, m2l(): pl.pallas_call(m2l_kernel, out_shape=jax.ShapeDtypeStruct((ne, 1024), BF)...  28.4 us

profile of v3, /device:TPU:1, one launch (start us, length us, event | category | flops | bytes accessed | tf_op | source)
XLA Modules:
  0.0 69.7 jit_solution(13589054437163790388)
XLA Ops:
  0.0 0.0 copy-start
  0.0 41.3 %shard_map.82 = (bf16[8,64,128]{2,1,0:T(8,128)(2,1)S(1)}, bf16[8,136,128]{2,1,0:T(8,128)(2,1)S(1)}, s32[320,128]{1,0:T(8,128)S(1)}) custom-call(s32[1,960]{1,0:T(1,128)} %g_hbm.1, bf16[294,1024]{1,0:T(8,128)(2,1)} %x_hbm.1, bf16[294,8,294]{2,1,0:T(8,128)(2,1)} %u_hbm.1, bf16[64,294]{1,0:T(8,128)(2,1)} %p_hbm.1, s32[316,128]{1,0:T(8,128)} %n_hbm.1), custom_call_target="tpu_custom_call" | custom-call | tf_op jit(solution)/shard_map/pallas_call | solution.py:188
  41.4 0.0 copy-done
  41.4 28.4 %shard_map.83 = bf16[294,1024]{1,0:T(8,128)(2,1)} custom-call(s32[320,128]{1,0:T(8,128)S(1)} %get-tuple-element.8.idx_ref, bf16[8,64,128]{2,1,0:T(8,128)(2,1)S(1)} %get-tuple-element.9.own_ref, bf16[8,136,128]{2,1,0:T(8,128)(2,1)S(1)} %get-tuple-element.10.gh_ref, bf16[64,20224]{1,0:T(8,128)(2,1)S(1)} %copy-done, bf16[64,294]{1,0:T(8,128)(2,1)} %bitcast.1, ...), custom_call_target="tpu_custom_call" | custom-call | tf_op jit(solution)/shard_map/pallas_call | solution.py:293
Async XLA Ops:
  0.0 41.4 %copy-start = (bf16[64,20224]{1,0:T(8,128)(2,1)S(1)}, bf16[64,20224]{1,0:T(8,128)(2,1)}, u32[]{:S(2)}) copy-start(bf16[64,20224]{1,0:T(8,128)(2,1)} %t_ref.1) | copy-start | bytes 7766020

commit v4 on v3

--- a/solution.py
+++ b/solution.py
@@ -36,22 +36,6 @@
     ne = u_ref.shape[0]
     barrier = pltpu.get_barrier_semaphore()
 
-    def grp_peer(d):
-        return lax.rem(me_g + d, n_grp)
-
-    def sub_peer(d):
-        return lax.rem(me_s + d, n_sub)
-
-    @pl.loop(1, n_grp)
-    def _(d):
-        pl.semaphore_signal(barrier, inc=1, device_id={"grp": grp_peer(d), "sub": me_s},
-                            device_id_type=pl.DeviceIdType.MESH)
-
-    @pl.loop(1, n_sub)
-    def _(d):
-        pl.semaphore_signal(barrier, inc=1, device_id={"grp": me_g, "sub": sub_peer(d)},
-                            device_id_type=pl.DeviceIdType.MESH)
-
     loads = [
         pltpu.make_async_copy(src, dst, in_sem.at[n])
         for n, (src, dst) in enumerate([(u_hbm, u_ref), (x_hbm, x_ref), (g_hbm, gs_ref),
@@ -59,6 +43,38 @@
     ]
     for load in loads:
         load.start()
+    n_z = 12
+    me_x, me_z, me_c = me_g // (2 * n_z), lax.rem(me_g // 2, n_z), lax.rem(me_g, 2)
+
+    def for_grp_peers(act):
+        n_x = n_grp // (2 * n_z)
+
+        def row(step, last):
+            half = (step + 1) // 2
+            z = lax.rem(me_z + n_z // 2 + half * (1 - 2 * lax.rem(step, 2)) + n_z, n_z)
+            for dx in sorted(range(n_x), key=lambda v: -min(v, n_x - v)):
+                for dc in (1, 0):
+                    if last and dx == 0 and dc == 0:
+                        continue
+                    x, c = lax.rem(me_x + dx, n_x), lax.rem(me_c + dc, 2)
+                    act((x * n_z + z) * 2 + c)
+
+        @pl.loop(0, n_z - 1)
+        def _(step):
+            row(step, False)
+
+        row(jnp.int32(n_z - 1), True)
+
+    def for_sub_peers(act):
+        for d in sorted(range(1, n_sub), key=lambda v: -min(v, n_sub - v)):
+            act(lax.rem(me_s + d, n_sub))
+
+    def greet(g, s):
+        pl.semaphore_signal(barrier, inc=1, device_id={"grp": g, "sub": s},
+                            device_id_type=pl.DeviceIdType.MESH)
+
+    for_grp_peers(lambda g: greet(g, me_s))
+    for_sub_peers(lambda s: greet(me_g, s))
     loads[0].wait()
     flat = u_ref[...].reshape(ne * 8, ne).astype(F32)
     starts = range(0, ne, 128)
@@ -85,39 +101,36 @@
     sf[...] = jnp.zeros_like(sf)
     loads[2].wait()
 
-    @pl.loop(0, n_grp)
-    def _(g):
-        for k in range(5):
-            sf[g, pl.ds(k, 1), :] = jnp.where(lo64, tab[pl.ds(gs_ref[0, g * 10 + k], 1), :],
-                                              tab[pl.ds(gs_ref[0, g * 10 + 5 + k], 1), :])
-
-    send[...] = sf[...].astype(BF)
+    @pl.loop(0, n_grp // 8)
+    def _(step):
+        for n in range(8):
+            g = step * 8 + n
+            for k in range(5):
+                sf[g, pl.ds(k, 1), :] = jnp.where(lo64, tab[pl.ds(gs_ref[0, g * 10 + k], 1), :],
+                                                  tab[pl.ds(gs_ref[0, g * 10 + 5 + k], 1), :])
+
+    for j in range(3):
+        send[:, j] = sf[:, 2 * j : 2 * j + 2, :].astype(BF)
     recv[me_g] = send[me_g]
     pl.semaphore_wait(barrier, n_grp + n_sub - 2)
 
-    def own_copy(d):
+    def own_copy(s):
         return pltpu.make_async_remote_copy(
             src_ref=own, dst_ref=ownr.at[me_s], send_sem=own_send, recv_sem=own_recv,
-            device_id={"grp": me_g, "sub": sub_peer(d)}, device_id_type=pl.DeviceIdType.MESH)
-
-    def slot_copy(d):
-        g = grp_peer(d)
+            device_id={"grp": me_g, "sub": s}, device_id_type=pl.DeviceIdType.MESH)
+
+    def slot_copy(g):
         return pltpu.make_async_remote_copy(
             src_ref=send.at[g], dst_ref=recv.at[me_g], send_sem=slot_send, recv_sem=slot_recv,
             device_id={"grp": g, "sub": me_s}, device_id_type=pl.DeviceIdType.MESH)
 
-    def gh_copy(d):
+    def gh_copy(s):
         return pltpu.make_async_remote_copy(
             src_ref=comp, dst_ref=ghr.at[me_s], send_sem=gh_send, recv_sem=gh_recv,
-            device_id={"grp": me_g, "sub": sub_peer(d)}, device_id_type=pl.DeviceIdType.MESH)
-
-    @pl.loop(1, n_grp)
-    def _(d):
-        slot_copy(d).start()
-
-    @pl.loop(1, n_sub)
-    def _(d):
-        own_copy(d).start()
+            device_id={"grp": me_g, "sub": s}, device_id_type=pl.DeviceIdType.MESH)
+
+    for_grp_peers(lambda g: slot_copy(g).start())
+    for_sub_peers(lambda s: own_copy(s).start())
 
     def iota(shape, dim):
         return lax.broadcasted_iota(I32, shape, dim)
@@ -143,33 +156,34 @@
 
     loads[5].wait()
     offs = nbr_ref.shape[0]
-    tail = offs % 8
-    idx_out[pl.ds(0, 8), :] = jnp.concatenate(
-        [place(nbr_ref[pl.ds(0, tail), :], ranks), jnp.full((8 - tail, 128), ZERO_ROW, I32)], axis=0)
-    for i in range(offs // 8):
-        idx_out[pl.ds(8 * i + 8, 8), :] = place(nbr_ref[pl.ds(tail + 8 * i, 8), :], ranks)
+    tail = offs % 16
+    idx_out[pl.ds(0, 8), :] = place(nbr_ref[pl.ds(0, 8), :], ranks)
+    idx_out[pl.ds(8, 8), :] = jnp.concatenate(
+        [place(nbr_ref[pl.ds(8, tail - 8), :], ranks), jnp.full((16 - tail, 128), ZERO_ROW, I32)], axis=0)
+    for i in range((offs - tail) // 8):
+        idx_out[pl.ds(8 * i + 16, 8), :] = place(nbr_ref[pl.ds(tail + 8 * i, 8), :], ranks)
 
     def all_slots(ref):
         return ref.at[pl.ds(0, n_grp - 1)]
 
     every_slot = pltpu.make_async_remote_copy(
         src_ref=all_slots(send), dst_ref=all_slots(recv), send_sem=slot_send, recv_sem=slot_recv,
-        device_id={"grp": grp_peer(1), "sub": me_s}, device_id_type=pl.DeviceIdType.MESH)
+        device_id={"grp": lax.rem(me_g + 1, n_grp), "sub": me_s}, device_id_type=pl.DeviceIdType.MESH)
     every_slot.wait_recv()
-    got = recv[...].astype(F32).reshape(n_grp * 8, 128).astype(BF)
+    for j in range(3):
+        sf[:, 2 * j : 2 * j + 2, :] = recv[:, j].astype(F32)
+    got = sf[...].reshape(n_grp * 8, 128).astype(BF)
     packed_ghosts = jnp.dot(hot[...], got, preferred_element_type=F32).astype(BF)
     comp[...] = packed_ghosts
     ghr[me_s] = packed_ghosts
 
-    @pl.loop(1, n_sub)
-    def _(d):
-        gh_copy(d).start()
+    for_sub_peers(lambda s: gh_copy(s).start())
 
     def every(ref, src, s_sem, r_sem):
         part = ref.at[pl.ds(0, n_sub - 1)]
         return pltpu.make_async_remote_copy(
             src_ref=part, dst_ref=part, send_sem=s_sem, recv_sem=r_sem,
-            device_id={"grp": me_g, "sub": sub_peer(1)}, device_id_type=pl.DeviceIdType.MESH)
+            device_id={"grp": me_g, "sub": lax.rem(me_s + 1, n_sub)}, device_id_type=pl.DeviceIdType.MESH)
 
     every_own = every(ownr, own, own_send, own_recv)
     every_own.wait_recv()
@@ -205,8 +219,8 @@
             pltpu.VMEM((pl.cdiv(ne, 128), ne * 8, 128), F32),
             pltpu.VMEM((136, 128), F32),
             pltpu.VMEM((n_grp, 8, 128), F32),
-            pltpu.VMEM((n_grp, 8, 128), BF),
-            pltpu.VMEM((n_grp, 8, 128), BF),
+            pltpu.VMEM((n_grp, 3, 2, 128), BF),
+            pltpu.VMEM((n_grp, 3, 2, 128), BF),
             pltpu.VMEM((64, 128), BF),
             pltpu.VMEM((n_sub, 64, 128), BF),
             pltpu.VMEM((GH_ROWS, 128), BF),
@@ -221,17 +235,17 @@
 
 
 def m2l_kernel(idx_ref, own_ref, gh_ref, t_ref, e_hbm, d_hbm, out_ref,
-               tab, e_ref, d_ref, late_sem, sem, acc, dsc, *bufs):
+               tab, flat, e_ref, d_ref, late_sem, sem, acc, dsc, *bufs):
     sms, sts = bufs[:BUF], bufs[BUF:]
-    full = idx_ref.shape[0] // 8 - 1
-    tail = t_ref.shape[1] // 64 - 8 * full
+    chunks = idx_ref.shape[0] // 16
+    tiles = tab.shape[0] // 256
     e_load = pltpu.make_async_copy(e_hbm, e_ref, late_sem.at[0])
     d_load = pltpu.make_async_copy(d_hbm, d_ref, late_sem.at[1])
     e_load.start()
     d_load.start()
 
     def fetch(i, b):
-        return pltpu.make_async_copy(idx_ref.at[pl.ds(pl.multiple_of(i * 8, 8), 8)], sms[b], sem.at[b])
+        return pltpu.make_async_copy(idx_ref.at[pl.ds(pl.multiple_of(i * 16, 16), 8)], sms[b], sem.at[b])
 
     for b in range(BUF):
         fetch(b, b).start()
@@ -240,43 +254,64 @@
     def spread(src, base, rows):
         x = src.astype(F32)
         y = pltpu.roll(x, 64, 1)
-        tab[pl.ds(pl.multiple_of(base, 8), rows), :] = jnp.where(lo64, x, y)
-        tab[pl.ds(pl.multiple_of(base + rows, 8), rows), :] = jnp.where(lo64, y, x)
+        tab[pl.ds(base, rows), :] = jnp.where(lo64, x, y)
+        tab[pl.ds(base + rows, rows), :] = jnp.where(lo64, y, x)
 
     for s in range(8):
         spread(own_ref[s], s * 128, 64)
         spread(gh_ref[s], 1024 + s * 2 * GH_ROWS, GH_ROWS)
-    tab[pl.ds(ZERO_ROW, 8), :] = jnp.zeros((8, 128), F32)
+    rest = tab.shape[0] - ZERO_ROW
+    tab[pl.ds(ZERO_ROW, rest), :] = jnp.zeros((rest, 128), F32)
+    for h in range(tiles):
+        flat[pl.ds(h * 64, 64), :] = tab[pl.ds(h * 256, 256), :].T[:64].astype(BF)
     acc[...] = jnp.zeros_like(acc)
 
-    def gather(sm, st, rows):
-        for o in range(0, rows, 2):
+    def by_rows(sm, st, first):
+        for o in range(0, 8, 2):
             for t in range(128):
                 st[o // 2, pl.ds(t, 1), :] = jnp.where(
                     lo64, tab[pl.ds(sm[o, t], 1), :], tab[pl.ds(sm[o + 1, t], 1), :])
-
-    def product(first, st, rows):
-        p = jnp.concatenate([st[j] for j in range(rows // 2)], axis=1).astype(BF)
-        tt = t_ref[:, pl.ds(pl.multiple_of(first * 64, 256), rows * 64)]
-        acc[...] += lax.dot_general(tt, p, NT, preferred_element_type=F32)
-
-    fetch(0, 0).wait()
-    gather(sms[0], sts[0], tail)
-    product(0, sts[0], tail)
+        p = jnp.concatenate([st[j] for j in range(4)], axis=1).astype(BF)
+        return lax.dot_general(t_ref[:, pl.ds(pl.multiple_of(first * 64, 256), 512)], p, NT,
+                               preferred_element_type=F32)
+
+    def by_select(row, first, count):
+        block = idx_ref[pl.ds(pl.multiple_of(row, 8), 8), :]
+        deep = lax.broadcasted_iota(I32, (256, 256), 0)
+        parts = []
+        for o in range(0, count, 2):
+            v = jnp.concatenate([block[o : o + 1], block[o + 1 : o + 2]], axis=1)
+            low, high = v & 255, v >> 8
+            hot = jnp.where(deep == low, 1.0, 0.0).astype(BF)
+            every = jnp.dot(flat[...], hot, preferred_element_type=F32)
+            got = jnp.where(high == 0, every[0:64], 0.0)
+            for h in range(1, tiles):
+                got = jnp.where(high == h, every[h * 64 : h * 64 + 64], got)
+            got = got.astype(BF)
+            parts += [got[:, :128], got[:, 128:]]
+        return jnp.dot(t_ref[:, pl.ds(pl.multiple_of(first * 64, 256), count * 64)],
+                       jnp.concatenate(parts, axis=0), preferred_element_type=F32)
+
+    def chunk(i, b, first, count=8):
+        fetch(i, b).wait()
+        acc[...] += by_rows(sms[b], sts[b], first) + by_select(16 * i + 8, first + 8, count)
+
+    tail = t_ref.shape[1] // 64 - 16 * (chunks - 1)
+    chunk(0, 0, 0, tail - 8)
     fetch(BUF, 0).start()
-
-    @pl.loop(0, full // BUF)
+    chunk(1, 1, tail)
+    fetch(BUF + 1, 1).start()
+
+    @pl.loop(0, (chunks - 2) // BUF)
     def _(j):
         for c in range(BUF):
-            b = (c + 1) % BUF
-            i = BUF * j + c
-            fetch(i + 1, b).wait()
-            gather(sms[b], sts[b], 8)
-            product(tail + 8 * i, sts[b], 8)
-
-            @pl.when(i + 1 + BUF <= full)
+            b = (c + 2) % BUF
+            i = BUF * j + c + 2
+            chunk(i, b, tail + 16 * (i - 1))
+
+            @pl.when(i + BUF < chunks)
             def _():
-                fetch(i + 1 + BUF, b).start()
+                fetch(i + BUF, b).start()
 
     lc = acc[...].astype(BF)
     e_load.wait()
@@ -290,13 +325,15 @@
 
 def m2l(idx, own, gh, t, e, d):
     ne = d.shape[0]
+    table = pl.cdiv(ZERO_ROW + 1, 256) * 256
     return pl.pallas_call(
         m2l_kernel,
         out_shape=jax.ShapeDtypeStruct((ne, 1024), BF),
-        in_specs=[pl.BlockSpec(memory_space=pl.ANY)] + [VM] * 3 + [HB] * 2,
+        in_specs=[VM] * 4 + [HB] * 2,
         out_specs=VM,
         scratch_shapes=[
-            pltpu.VMEM((1024 + 16 * GH_ROWS + 8, 128), F32),
+            pltpu.VMEM((table, 128), F32),
+            pltpu.VMEM((table // 4, 256), BF),
             pltpu.VMEM(e.shape[::-1], BF),
             pltpu.VMEM(d.shape, BF),
             pltpu.SemaphoreType.DMA((2,)),

time: 70.2 us -> 63.2 us (0.900)
  Pallas kernels: 69.7 us -> 63 us
    pallas_call x1, Pallas kernels: 41.3 us -> 36.7 us  [exchange(): pl.pallas_call(functools.partial(exchange_kernel, n_grp, n_sub), out_shap...]
    pallas_call x1, Pallas kernels: 28.4 us -> 26.4 us  [m2l(): pl.pallas_call(m2l_kernel, out_shape=jax.ShapeDtypeStruct((ne, 1024), BF)...]
where the time goes in v4:
time: 63.2 us; the launch traced here: 63 us
  Pallas kernels  63 us (100%)
    pallas_call x1, Pallas kernels, exchange(): pl.pallas_call(functools.partial(exchange_kernel, n_grp, n_sub), out_shap...  36.7 us
    pallas_call x1, Pallas kernels, m2l(): pl.pallas_call(m2l_kernel, out_shape=jax.ShapeDtypeStruct((ne, 1024), BF)...  26.4 us

profile of v4, /device:TPU:1, one launch (start us, length us, event | category | flops | bytes accessed | tf_op | source)
XLA Modules:
  0.0 63.0 jit_solution(11034178361902941829)
XLA Ops:
  0.0 0.0 copy-start
  0.0 36.7 %shard_map.82 = (bf16[8,64,128]{2,1,0:T(8,128)(2,1)S(1)}, bf16[8,136,128]{2,1,0:T(8,128)(2,1)S(1)}, s32[320,128]{1,0:T(8,128)S(1)}) custom-call(s32[1,960]{1,0:T(1,128)} %g_hbm.1, bf16[294,1024]{1,0:T(8,128)(2,1)} %x_hbm.1, bf16[294,8,294]{2,1,0:T(8,128)(2,1)} %u_hbm.1, bf16[64,294]{1,0:T(8,128)(2,1)} %p_hbm.1, s32[316,128]{1,0:T(8,128)} %n_hbm.1), custom_call_target="tpu_custom_call" | custom-call | tf_op jit(solution)/shard_map/pallas_call | solution.py:202
  36.7 0.0 copy-done
  36.7 26.4 %shard_map.83 = bf16[294,1024]{1,0:T(8,128)(2,1)} custom-call(s32[320,128]{1,0:T(8,128)S(1)} %get-tuple-element.8.idx_ref, bf16[8,64,128]{2,1,0:T(8,128)(2,1)S(1)} %get-tuple-element.9.own_ref, bf16[8,136,128]{2,1,0:T(8,128)(2,1)S(1)} %get-tuple-element.10.gh_ref, bf16[64,20224]{1,0:T(8,128)(2,1)S(1)} %copy-done, bf16[64,294]{1,0:T(8,128)(2,1)} %bitcast.1, ...), custom_call_target="tpu_custom_call" | custom-call | tf_op jit(solution)/shard_map/pallas_call | solution.py:329
Async XLA Ops:
  0.0 36.7 %copy-start = (bf16[64,20224]{1,0:T(8,128)(2,1)S(1)}, bf16[64,20224]{1,0:T(8,128)(2,1)}, u32[]{:S(2)}) copy-start(bf16[64,20224]{1,0:T(8,128)(2,1)} %t_ref.1) | copy-start | bytes 7766020

commit v5 on v4

--- a/solution.py
+++ b/solution.py
@@ -29,8 +29,8 @@
     return jnp.where(v >= 8704, ZERO_ROW, row)
 
 
-def exchange_kernel(n_grp, n_sub, g_hbm, x_hbm, u_hbm, p_hbm, n_hbm, own_out, gh_out, idx_out,
-                    gs_ref, gv_ref, x_ref, u_ref, p_ref, nbr_ref, in_sem, uf, tab, sf, send, recv, own, ownr, comp, ghr, hot,
+def exchange_kernel(n_grp, n_sub, g_hbm, x_hbm, u_hbm, p_hbm, n_hbm, own_out, gh_out, idx_out, part_out,
+                    gs_ref, gv_ref, x_ref, u_ref, p_ref, nbr_ref, in_sem, uf, tab, sf, send, recv, own, ownr, comp, ghr, hot, own_flat,
                     own_send, own_recv, slot_send, slot_recv, gh_send, gh_recv):
     me_g, me_s = lax.axis_index("grp"), lax.axis_index("sub")
     ne = u_ref.shape[0]
@@ -188,6 +188,25 @@
     every_own = every(ownr, own, own_send, own_recv)
     every_own.wait_recv()
     own_out[...] = ownr[...]
+    for h in range(4):
+        turned = [ownr[s].astype(F32).T for s in (2 * h, 2 * h + 1)]
+        own_flat[pl.ds(h * 64, 64), :] = jnp.concatenate(
+            [t[at : at + 64] for t in turned for at in (0, 64)], axis=1).astype(BF)
+
+    @pl.loop(0, idx_out.shape[0] // 16)
+    def _(i):
+        block = idx_out[pl.ds(pl.multiple_of(16 * i + 8, 8), 8), :]
+        deep = iota((256, 256), 0)
+        for o in range(0, 8, 2):
+            v = jnp.concatenate([block[o : o + 1], block[o + 1 : o + 2]], axis=1)
+            low, high = v & 255, v >> 8
+            chosen = jnp.where(deep == low, 1.0, 0.0).astype(BF)
+            each = jnp.dot(own_flat[...], chosen, preferred_element_type=F32)
+            got = jnp.where(high == 0, each[0:64], 0.0)
+            for h in range(1, 4):
+                got = jnp.where(high == h, each[h * 64 : h * 64 + 64], got)
+            part_out[i, :, pl.ds(o * 128, 256)] = got.astype(BF)
+
     every_slot.wait_send()
     every_own.wait_send()
     every_gh = every(ghr, comp, gh_send, gh_recv)
@@ -205,9 +224,10 @@
             jax.ShapeDtypeStruct((n_sub, 64, 128), BF),
             jax.ShapeDtypeStruct((n_sub, GH_ROWS, 128), BF),
             jax.ShapeDtypeStruct((320, 128), I32),
+            jax.ShapeDtypeStruct((20, 64, 1024), BF),
         ),
         in_specs=[HB] * 5,
-        out_specs=(VM, VM, VM),
+        out_specs=(VM, VM, VM, VM),
         scratch_shapes=[
             pltpu.SMEM(ghost_map.shape, I32),
             pltpu.VMEM(ghost_map.shape, I32),
@@ -226,6 +246,7 @@
             pltpu.VMEM((GH_ROWS, 128), BF),
             pltpu.VMEM((n_sub, GH_ROWS, 128), BF),
             pltpu.VMEM((GH_ROWS, n_grp * 8), BF),
+            pltpu.VMEM((256, 256), BF),
         ] + [dma] * 6,
         compiler_params=pltpu.CompilerParams(
             collective_id=0, has_side_effects=True, vmem_limit_bytes=24 * 2**20),
@@ -234,11 +255,11 @@
 BUF = 3
 
 
-def m2l_kernel(idx_ref, own_ref, gh_ref, t_ref, e_hbm, d_hbm, out_ref,
+def m2l_kernel(idx_ref, own_ref, gh_ref, part_ref, t_ref, e_hbm, d_hbm, out_ref,
                tab, flat, e_ref, d_ref, late_sem, sem, acc, dsc, *bufs):
     sms, sts = bufs[:BUF], bufs[BUF:]
     chunks = idx_ref.shape[0] // 16
-    tiles = tab.shape[0] // 256
+    tiles = tab.shape[0] // 256 - 4
     e_load = pltpu.make_async_copy(e_hbm, e_ref, late_sem.at[0])
     d_load = pltpu.make_async_copy(d_hbm, d_ref, late_sem.at[1])
     e_load.start()
@@ -263,7 +284,7 @@
     rest = tab.shape[0] - ZERO_ROW
     tab[pl.ds(ZERO_ROW, rest), :] = jnp.zeros((rest, 128), F32)
     for h in range(tiles):
-        flat[pl.ds(h * 64, 64), :] = tab[pl.ds(h * 256, 256), :].T[:64].astype(BF)
+        flat[pl.ds(h * 64, 64), :] = tab[pl.ds(1024 + h * 256, 256), :].T[:64].astype(BF)
     acc[...] = jnp.zeros_like(acc)
 
     def by_rows(sm, st, first):
@@ -275,8 +296,8 @@
         return lax.dot_general(t_ref[:, pl.ds(pl.multiple_of(first * 64, 256), 512)], p, NT,
                                preferred_element_type=F32)
 
-    def by_select(row, first, count):
-        block = idx_ref[pl.ds(pl.multiple_of(row, 8), 8), :]
+    def by_select(i, first, count):
+        block = idx_ref[pl.ds(pl.multiple_of(16 * i + 8, 8), 8), :]
         deep = lax.broadcasted_iota(I32, (256, 256), 0)
         parts = []
         for o in range(0, count, 2):
@@ -284,9 +305,9 @@
             low, high = v & 255, v >> 8
             hot = jnp.where(deep == low, 1.0, 0.0).astype(BF)
             every = jnp.dot(flat[...], hot, preferred_element_type=F32)
-            got = jnp.where(high == 0, every[0:64], 0.0)
-            for h in range(1, tiles):
-                got = jnp.where(high == h, every[h * 64 : h * 64 + 64], got)
+            got = part_ref[i, :, pl.ds(o * 128, 256)].astype(F32)
+            for h in range(tiles):
+                got = jnp.where(high == h + 4, every[h * 64 : h * 64 + 64], got)
             got = got.astype(BF)
             parts += [got[:, :128], got[:, 128:]]
         return jnp.dot(t_ref[:, pl.ds(pl.multiple_of(first * 64, 256), count * 64)],
@@ -294,7 +315,7 @@
 
     def chunk(i, b, first, count=8):
         fetch(i, b).wait()
-        acc[...] += by_rows(sms[b], sts[b], first) + by_select(16 * i + 8, first + 8, count)
+        acc[...] += by_rows(sms[b], sts[b], first) + by_select(i, first + 8, count)
 
     tail = t_ref.shape[1] // 64 - 16 * (chunks - 1)
     chunk(0, 0, 0, tail - 8)
@@ -323,17 +344,17 @@
         out_ref[:, c * 128 : (c + 1) * 128] = dsc[pl.ds(c, ne, stride=8), :].astype(BF)
 
 
-def m2l(idx, own, gh, t, e, d):
+def m2l(idx, own, gh, part, t, e, d):
     ne = d.shape[0]
     table = pl.cdiv(ZERO_ROW + 1, 256) * 256
     return pl.pallas_call(
         m2l_kernel,
         out_shape=jax.ShapeDtypeStruct((ne, 1024), BF),
-        in_specs=[VM] * 4 + [HB] * 2,
+        in_specs=[VM] * 5 + [HB] * 2,
         out_specs=VM,
         scratch_shapes=[
             pltpu.VMEM((table, 128), F32),
-            pltpu.VMEM((table // 4, 256), BF),
+            pltpu.VMEM((table // 4 - 256, 256), BF),
             pltpu.VMEM(e.shape[::-1], BF),
             pltpu.VMEM(d.shape, BF),
             pltpu.SemaphoreType.DMA((2,)),
@@ -344,7 +365,7 @@
             *[pltpu.VMEM((4, 128, 128), F32)] * BUF,
         ],
         compiler_params=pltpu.CompilerParams(vmem_limit_bytes=24 * 2**20),
-    )(idx, own, gh, t, *[pltpu.with_memory_space_constraint(a, pltpu.HBM) for a in (e.T, d)])
+    )(idx, own, gh, part, t, *[pltpu.with_memory_space_constraint(a, pltpu.HBM) for a in (e.T, d)])
 
 
 def on_device(
@@ -357,9 +378,9 @@
     neighbour_list,
     ghost_map,
 ):
-    own, ghosts, index = exchange(ghost_map, child_moments, upward_matrix, project_matrix,
+    own, ghosts, index, part = exchange(ghost_map, child_moments, upward_matrix, project_matrix,
                                   neighbour_list, lax.axis_size("grp"), lax.axis_size("sub"))
-    return m2l(index, own, ghosts, transfer_matrix, expand_matrix, downward_matrix)
+    return m2l(index, own, ghosts, part, transfer_matrix, expand_matrix, downward_matrix)
 
 
 def solution(mesh):

time: 63.2 us -> 61.4 us (0.972)
  Pallas kernels: 63 us -> 61.2 us
    pallas_call x1, Pallas kernels: 26.4 us -> 24.6 us  [m2l(): pl.pallas_call(m2l_kernel, out_shape=jax.ShapeDtypeStruct((ne, 1024), BF)...]
where the time goes in v5:
time: 61.4 us; the launch traced here: 61.3 us
  Pallas kernels  61.2 us (100%)
    pallas_call x1, Pallas kernels, exchange(): pl.pallas_call(functools.partial(exchange_kernel, n_grp, n_sub), out_shap...  36.7 us
    pallas_call x1, Pallas kernels, m2l(): pl.pallas_call(m2l_kernel, out_shape=jax.ShapeDtypeStruct((ne, 1024), BF)...  24.6 us

profile of v5, /device:TPU:1, one launch (start us, length us, event | category | flops | bytes accessed | tf_op | source)
XLA Modules:
  0.0 61.3 jit_solution(2710223080559869291)
XLA Ops:
  0.0 0.0 copy-start
  0.0 36.7 %shard_map.82 = (bf16[8,64,128]{2,1,0:T(8,128)(2,1)S(1)}, bf16[8,136,128]{2,1,0:T(8,128)(2,1)S(1)}, s32[320,128]{1,0:T(8,128)S(1)}, bf16[20,64,1024]{2,1,0:T(8,128)(2,1)S(1)}) custom-call(s32[1,960]{1,0:T(1,128)} %g_hbm.1, bf16[294,1024]{1,0:T(8,128)(2,1)} %x_hbm.1, bf16[294,8,294]{2,1,0:T(8,128)(2,1)} %u_hbm.1, bf16[64,294]{1,0:T(8,128)(2,1)} %p_hbm.1, ...), custom_call_target="tpu_custom_call" | custom-call | tf_op jit(solution)/shard_map/pallas_call | solution.py:221
  36.7 0.0 copy-done
  36.7 24.6 %shard_map.83 = bf16[294,1024]{1,0:T(8,128)(2,1)} custom-call(s32[320,128]{1,0:T(8,128)S(1)} %get-tuple-element.9.idx_ref, bf16[8,64,128]{2,1,0:T(8,128)(2,1)S(1)} %get-tuple-element.10.own_ref, bf16[8,136,128]{2,1,0:T(8,128)(2,1)S(1)} %get-tuple-element.11.gh_ref, bf16[20,64,1024]{2,1,0:T(8,128)(2,1)S(1)} %get-tuple-element.12.part_ref, ...), custom_call_target="tpu_custom_call" | custom-call | tf_op jit(solution)/shard_map/pallas_call | solution.py:350
Async XLA Ops:
  0.0 36.7 %copy-start = (bf16[64,20224]{1,0:T(8,128)(2,1)S(1)}, bf16[64,20224]{1,0:T(8,128)(2,1)}, u32[]{:S(2)}) copy-start(bf16[64,20224]{1,0:T(8,128)(2,1)} %t_ref.1) | copy-start | bytes 7766020
